TPU v7x, 32 devices: a whole 2x2x4 slice. The times are simulated.
32 devices in a mesh: layer: 8 (over y, x, core), tensor: 4 (over z).
Axes of the slice: x: 2, y: 2, z: 4, core: 2. Of those that a mesh axis runs over, the one named last changes fastest.
Arguments:
- gradient: bfloat16 [8, 1024, 8192], P(None, 'tensor', 'layer'), may hold values from -8 to 8
- row_basis: bfloat16 [8, 1024, 256], P('layer', 'tensor'), may hold values from -0.1875 to 0.1875
- column_basis: bfloat16 [8, 8192, 256], P('layer', 'tensor'), may hold values from -0.0625 to 0.0625
- row_eigen: float32 [8, 256], P('layer'), may hold values from 0.01 to 10
- column_eigen: float32 [8, 256], P('layer'), may hold values from 0.01 to 10
- row_escape: float32 [8], P('layer'), may hold values from 0.02 to 0.2
- column_escape: float32 [8], P('layer'), may hold values from 0.02 to 0.2
Outputs:
- update: bfloat16 [8, 1024, 8192], P(None, 'tensor', 'layer')
All inputs are finite; a program needn't handle non-finite values.
Results may differ from a plain program's by a relative error of at most 0.0055.
Values may be sent and summed in bfloat16 or wider, within the bound.
A program may use at most 128 MiB of HBM per device.

v0:
```python
import jax
import jax.numpy as jnp
from jax import lax
from jax.sharding import PartitionSpec as P


def coefficients(row_eigen, column_eigen, row_escape, column_escape):
    row_base = row_escape ** (-0.25)
    column_base = column_escape ** (-0.25)
    row_coef = (row_eigen + row_escape[:, None]) ** (-0.25) - row_base[:, None]
    column_coef = (column_eigen + column_escape[:, None]) ** (-0.25) - column_base[:, None]
    return (row_base, column_base, row_coef, column_coef)


def group_norm(local_block):
    partial_sq = jnp.sum(jnp.square(local_block.astype(jnp.float32)), axis=(1, 2))
    return lax.psum(partial_sq, "tensor")


def finish(raw_update, grad_sq):
    update_sq = lax.psum(jnp.sum(jnp.square(raw_update), axis=(1, 2)), "tensor")
    factor = jnp.sqrt((grad_sq + 1.0) / (update_sq + 1.0))
    return (raw_update * factor[:, None, None]).astype(jnp.bfloat16)


def body(gradient, row_basis, column_basis, row_eigen, column_eigen, row_escape, column_escape):
    row_base, column_base, row_coef, column_coef = coefficients(
        row_eigen, column_eigen, row_escape, column_escape
    )
    both_base = (row_base * column_base)[:, None, None]
    group_block = lax.all_to_all(gradient, "layer", split_axis=0, concat_axis=2, tiled=True)
    grad_sq = group_norm(group_block)
    own_proj = lax.psum_scatter(
        jnp.einsum(
            "lrk,lrd->dlk", row_basis, group_block, preferred_element_type=jnp.float32
        ).astype(jnp.bfloat16),
        "tensor",
        scatter_dimension=0,
        tiled=True,
    ).astype(jnp.float32)
    scaled = (own_proj * row_coef[None]).astype(jnp.bfloat16)
    core_part = jnp.einsum("dlk,ldj->lkj", scaled, column_basis, preferred_element_type=jnp.float32)
    core_mat = lax.psum(core_part.astype(jnp.bfloat16), "tensor")
    whole_columns = lax.all_gather(column_basis, "tensor", axis=1, tiled=True)
    middle = jnp.einsum(
        "lrd,ldk->lrk", group_block, whole_columns, preferred_element_type=jnp.float32
    )
    row_term = jnp.einsum(
        "lrk,dlk->lrd",
        row_basis,
        lax.all_gather(scaled, "tensor", axis=0, tiled=True),
        preferred_element_type=jnp.float32,
    )
    mixed = row_base[:, None, None] * middle + jnp.einsum(
        "lrk,lkj->lrj", row_basis, core_mat, preferred_element_type=jnp.float32
    )
    left_factor = (mixed * column_coef[:, None, :]).astype(jnp.bfloat16)
    raw_update = both_base * group_block.astype(jnp.float32) + column_base[:, None, None] * row_term
    raw_update = raw_update + jnp.einsum(
        "lrk,ldk->lrd", left_factor, whole_columns, preferred_element_type=jnp.float32
    )
    rows_block = finish(raw_update, grad_sq)
    return lax.all_to_all(rows_block, "layer", split_axis=2, concat_axis=0, tiled=True)


def solution(mesh):
    in_specs = (
        P(None, "tensor", "layer"),
        P("layer", "tensor", None),
        P("layer", "tensor", None),
        P("layer", None),
        P("layer", None),
        P("layer"),
        P("layer"),
    )
    out_specs = P(None, "tensor", "layer")
    return jax.shard_map(body, mesh=mesh, in_specs=in_specs, out_specs=out_specs, check_vma=False)
```

profile of v0, /device:TPU:0, one launch (start us, length us, event | category | flops | bytes accessed | tf_op | source)
XLA Modules:
  0.0 558.4 jit_solution(9425964493506922182)
XLA Ops:
  6.5 0.0 copy-start
  6.5 0.0 reduce-scatter.2.cloned.1.call-start
  6.5 54.5 %all_to_all.36 = bf16[8,256,1024]{2,1,0:T(8,128)(2,1)} all-to-all(bf16[8,256,1024]{2,1,0:T(8,128)(2,1)} %param.7), channel_id=1, replica_groups=mesh['layer'=8,'tensor'=4] {'layer'}, dimensions={0} | all-to-all | bytes 8388608 | tf_op jit(solution)/shard_map/all_to_all | solution.py:31
  61.0 6.4 %copy.15 = bf16[1,256,8,1024]{1,3,2,0:T(8,128)(2,1)} copy(bf16[1,256,8,1024]{3,1,2,0:T(8,128)(2,1)} %bitcast.80) | data formatting | bytes 8388608 | tf_op jit(solution)/shard_map/all_to_all | solution.py:31
  67.4 0.0 copy-done
  67.4 5.4 fusion.2
  72.8 0.0 copy-start.4
  72.8 0.0 copy-start.5
  72.8 0.0 reduce-scatter.2.cloned.1.call-update
  72.9 0.0 all-gather.5.cloned.1.call-start
  72.9 0.7 all-gather.5.cloned.1.call-update
  73.6 0.0 all-gather.3.cloned.1.call-start
  74.4 0.0 copy-done.4
  74.4 75.4 %reduce-scatter.2.cloned.1.call-done = bf16[2048,1,256]{2,0,1:T(8,128)(2,1)} async-done(((bf16[8192,1,256]{2,0,1:T(8,128)(2,1)}), bf16[2048,1,256]{2,0,1:T(8,128)(2,1)}) %reduce-scatter.2.cloned.1.call-update) | async-done | bytes 1048592 | tf_op jit(solution)/shard_map/reduce_scatter | solution.py:33
  149.8 2.4 multiply_convert_fusion.1
  152.2 0.0 all-gather.3.cloned.1.call-update
  152.3 0.0 all-reduce.3.cloned.1.call-start
  153.0 0.0 copy-done.5
  153.0 4.9 multiply_reduce_fusion.1
  157.9 0.0 copy-start.2
  158.0 0.0 copy-start.3
  158.0 74.7 %all-gather.5.cloned.1.call-done = bf16[1,8192,256]{2,1,0:T(8,128)(2,1)} async-done(((bf16[1,2048,256]{2,1,0:T(8,128)(2,1)}), bf16[1,8192,256]{2,1,0:T(8,128)(2,1)}) %all-gather.5.cloned.1.call-update) | async-done | bytes 4194320 | tf_op jit(solution)/shard_map/all_gather | solution.py:44
  232.7 4.8 fusion.10
  237.4 0.0 copy-done.2
  237.4 0.0 copy-done.3
  237.5 1.1 convolution_convert_fusion.1
  238.6 0.0 all-reduce.3.cloned.1.call-update
  238.6 75.0 %all-gather.3.cloned.1.call-done = bf16[8192,1,256]{2,0,1:T(8,128)(2,1)} async-done(((bf16[2048,1,256]{2,0,1:T(8,128)(2,1)}), bf16[8192,1,256]{2,0,1:T(8,128)(2,1)}) %all-gather.3.cloned.1.call-update) | async-done | bytes 4194320 | tf_op jit(solution)/shard_map/all_gather | solution.py:51
  313.6 8.0 %fusion.1 = f32[256,8192]{0,1:T(8,128)} fusion(bf16[256,8192]{0,1:T(8,128)(2,1)} %bitcast.79, bf16[8192,1,256]{2,0,1:T(8,128)(2,1)} %all-gather.3.cloned.1.call-done, f32[]{:T(128)} %bitcast.4, f32[]{:T(128)} %bitcast, bf16[1,256,256]{2,1,0:T(8,128)(2,1)S(1)} %copy-done), kind=kOutput, calls=%fused_computation.3 | convolution fusion | flops 1082130432 | bytes 16908296 | tf_op jit(solution)/shard_map/lrk,dlk->lrd/dot_general | solution.py:48
  321.6 27.3 %all-reduce.3.cloned.1.call-done = bf16[256,256]{1,0:T(8,128)(2,1)} async-done(((bf16[256,256]{1,0:T(8,128)(2,1)}), bf16[256,256]{1,0:T(8,128)(2,1)}) %all-reduce.3.cloned.1.call-update) | async-done | bytes 131088 | tf_op jit(solution)/shard_map/psum | solution.py:43
  348.9 11.0 %multiply_reduce_fusion = (f32[]{:T(128)}, f32[256,8192]{0,1:T(8,128)}) fusion(f32[256,8192]{0,1:T(8,128)} %fusion.1, bf16[1,8192,256]{2,1,0:T(8,128)(2,1)} %all-gather.5.cloned.1.call-done, f32[256,256]{1,0:T(8,128)S(1)} %fusion.10, bf16[256,256]{1,0:T(8,128)(2,1)} %all-reduce.3.cloned.1.call-done, bf16[1,256,256]{2,1,0:T(8,128)(2,1)S(1)} %copy-done, ...), kind=kOutput, calls=%fused_computation.7 | convolution fusion | flops 1113784320 | bytes 21496836 | tf_op jit(solution)/shard_map/lrk,ldk->lrd/dot_general | solution.py:59
  359.9 11.3 %all-reduce = (f32[1]{0:T(128)}, f32[1]{0:T(128)}) all-reduce(f32[1]{0:T(128)} %bitcast.19, f32[1]{0:T(128)} %bitcast.20), channel_id=1, replica_groups=mesh['layer'=8,'tensor'=4] {'tensor'}, use_global_device_ids=true, to_apply=%region_3.0 | all-reduce | flops 2 | bytes 16 | tf_op jit(solution)/shard_map/psum | solution.py:17
  372.5 4.1 fusion.3
  376.5 49.5 %copy.24 = bf16[1,256,8192]{1,0,2:T(2,128)(2,1)} copy(bf16[1,256,8192]{1,2,0:T(8,128)(2,1)S(1)} %fusion.3) | data formatting | bytes 8388608 | tf_op jit(solution)/shard_map/convert_element_type | solution.py:23
  426.1 0.5 broadcast.23
  426.6 43.5 %reduce.4 = bf16[8192,256]{1,0:T(8,128)(2,1)} reduce(bf16[8192,1,256]{2,1,0:T(2,128)(2,1)} %bitcast.81, bf16[]{:T(256)} %broadcast.23), dimensions={1}, to_apply=%bitcast.74.reduce_sub_computation | reduce | bytes 8388610
  470.1 7.0 %reshape.90 = bf16[8,2,131072]{2,1,0:T(2,128)(2,1)} reshape(bf16[8192,256]{1,0:T(8,128)(2,1)} %reduce.4) | data formatting | bytes 8388608
  477.1 53.6 %all_to_all.37 = bf16[8,2,131072]{2,1,0:T(2,128)(2,1)} all-to-all(bf16[8,2,131072]{2,1,0:T(2,128)(2,1)} %reshape.90), channel_id=1, replica_groups=mesh['layer'=8,'tensor'=4] {'layer'}, dimensions={0} | all-to-all | bytes 8388608 | tf_op jit(solution)/shard_map/all_to_all | solution.py:63
  530.6 8.7 %reshape.91 = bf16[8192,1,256]{2,1,0:T(2,128)(2,1)} reshape(bf16[8,2,131072]{2,1,0:T(2,128)(2,1)} %all_to_all.37) | data formatting | bytes 8388608
  539.4 6.1 %copy.22 = bf16[1,256,8192]{1,2,0:T(8,128)(2,1)} copy(bf16[1,256,8192]{1,0,2:T(2,128)(2,1)} %bitcast.82) | data formatting | bytes 8388608
  545.4 0.0 copy-start.1
  545.4 6.5 %copy.19 = bf16[8,256,1024]{2,1,0:T(8,128)(2,1)} copy(bf16[8,256,1024]{1,2,0:T(8,128)(2,1)} %bitcast.83) | data formatting | bytes 8388608 | tf_op jit(solution)/shard_map/all_to_all | solution.py:63
  551.9 0.0 copy-done.1
  (2 shorter events, 0.0 us)
Async XLA Ops:
  6.5 60.9 %copy-start = (bf16[1,256,256]{2,1,0:T(8,128)(2,1)S(1)}, bf16[1,256,256]{2,1,0:T(8,128)(2,1)}, u32[]{:S(2)}) copy-start(bf16[1,256,256]{2,1,0:T(8,128)(2,1)} %param.8) | copy-start | bytes 393220
  6.5 143.3 %reduce-scatter.2.cloned.1.call-start = ((), (), s32[]{:S(2)}) async-start(), calls=%async_computation.3 | async-start | bytes 5242880 | tf_op jit(solution)/shard_map/reduce_scatter | solution.py:33
  72.8 1.5 copy-start.4
  72.8 80.2 %copy-start.5 = (f32[1,256]{1,0:T(1,128)S(1)}, f32[1,256]{1,0:T(1,128)}, u32[]{:S(2)}) copy-start(f32[1,256]{1,0:T(1,128)} %param.11) | copy-start | bytes 3076
  72.9 159.8 %all-gather.5.cloned.1.call-start = ((), (), s32[]{:S(2)}) async-start(), calls=%async_computation.5 | async-start | bytes 5242880 | tf_op jit(solution)/shard_map/all_gather | solution.py:44
  73.6 239.9 %all-gather.3.cloned.1.call-start = ((), (), s32[]{:S(2)}) async-start(), calls=%async_computation.4 | async-start | bytes 5242880 | tf_op jit(solution)/shard_map/all_gather | solution.py:51
  152.3 196.6 %all-reduce.3.cloned.1.call-start = ((), (), s32[]{:S(2)}) async-start(), calls=%async_computation.6 | async-start | bytes 262144 | tf_op jit(solution)/shard_map/psum | solution.py:43
  157.9 79.5 %copy-start.2 = (bf16[2048,1,256]{2,0,1:T(8,128)(2,1)S(1)}, bf16[2048,1,256]{2,0,1:T(8,128)(2,1)}, u32[]{:S(2)}) copy-start(bf16[2048,1,256]{2,0,1:T(8,128)(2,1)} %multiply_convert_fusion.1) | copy-start | bytes 3145732
  158.0 79.5 %copy-start.3 = (bf16[1,2048,256]{2,1,0:T(8,128)(2,1)S(1)}, bf16[1,2048,256]{2,1,0:T(8,128)(2,1)}, u32[]{:S(2)}) copy-start(bf16[1,2048,256]{2,1,0:T(8,128)(2,1)} %param.9) | copy-start | bytes 3145732
  545.4 6.5 %copy-start.1 = (bf16[1,256,256]{2,1,0:T(8,128)(2,1)S(1)}, bf16[1,256,256]{2,1,0:T(8,128)(2,1)}, u32[]{:S(2)}) copy-start(bf16[1,256,256]{2,1,0:T(8,128)(2,1)} %param.8) | copy-start | bytes 393220
Sparse Core Ops, SparseCore 0:
  73.0 76.7 reduce-scatter.1
  151.4 81.2 all-gather.4
  234.3 79.2 all-gather.2
  315.7 33.1 all-reduce.2
where the time goes:
time: 559 us; the launch traced here: 558 us
  waiting for transfers between devices  253 us (45%)
  blocking collectives  119 us (21%)
  local copies, waits for them, and re-layouts  84.7 us (15%)
  other arithmetic  54.9 us (10%)
  matrix products  30.3 us (5%)
  between operations  15.9 us (3%)
    reduce_scatter x1, waiting for transfers between devices, body(): lax.psum_scatter(jnp.einsum('lrk,lrd->dlk', row_basis, group_block, prefe...  75.4 us
    all_gather x1, waiting for transfers between devices, body(): lax.all_gather(scaled, 'tensor', axis=0, tiled=True)  75 us
    all_gather x1, waiting for transfers between devices, body(): whole_columns = lax.all_gather(column_basis, 'tensor', axis=1, tiled=True)  74.7 us
    all_to_all x1, blocking collectives, body(): lax.all_to_all(gradient, 'layer', split_axis=0, concat_axis=2, tiled=True)  54.5 us
    all_to_all x1, blocking collectives, body(): lax.all_to_all(rows_block, 'layer', split_axis=2, concat_axis=0, tiled=True)  53.6 us
    convert_element_type x1, local copies, waits for them, and re-layouts, finish(): return (raw_update * factor[:, None, None]).astype(jnp.bfloat16)  49.5 us
    unnamed x1, other arithmetic  43.5 us
    psum x1, waiting for transfers between devices, body(): core_mat = lax.psum(core_part.astype(jnp.bfloat16), 'tensor')  27.3 us
  transfers between devices with their start and end apart: 4, of which 4 were waited for; matrix products, arithmetic and copies ran while one was open for 4% of the time, Pallas kernels for 0%

commit v1 on v0

--- a/solution.py
+++ b/solution.py
@@ -2,6 +2,23 @@
 import jax.numpy as jnp
 from jax import lax
 from jax.sharding import PartitionSpec as P
+
+
+def in_order(pieces, dim):
+    pieces = jnp.moveaxis(pieces, 0, dim)
+    lengths = pieces.shape
+    return pieces.reshape(*lengths[:dim], lengths[dim] * lengths[dim + 1], *lengths[dim + 2 :])
+
+
+def gather_around(value, axis, dim):
+    devices = lax.axis_size(axis)
+    right = [(i, (i + 1) % devices) for i in range(devices)]
+    blocks = [value]
+    while len(blocks) < devices:
+        blocks.append(lax.ppermute(blocks[-1], axis, right))
+    index = lax.axis_index(axis)
+    blocks = jnp.stack(blocks)[(index - jnp.arange(devices)) % devices]
+    return in_order(blocks, dim)
 
 
 def coefficients(row_eigen, column_eigen, row_escape, column_escape):
@@ -48,7 +65,7 @@
     row_term = jnp.einsum(
         "lrk,dlk->lrd",
         row_basis,
-        lax.all_gather(scaled, "tensor", axis=0, tiled=True),
+        gather_around(scaled, "tensor", 0),
         preferred_element_type=jnp.float32,
     )
     mixed = row_base[:, None, None] * middle + jnp.einsum(

time: 559 us -> 522 us (0.934)
  waiting for transfers between devices: 253 us -> 175 us
  starting transfers between devices: 0.12 us -> 32.8 us
    ppermute x0 -> x3, waiting for transfers between devices: none -> 96.5 us  [gather_around(): blocks.append(lax.ppermute(blocks[-1], axis, right))]
    all_gather x1 -> x0, waiting for transfers between devices: 75 us -> none  [body(): lax.all_gather(scaled, 'tensor', axis=0, tiled=True)]
    all_gather x1, waiting for transfers between devices: 74.7 us -> 1.01 us  [body(): whole_columns = lax.all_gather(column_basis, 'tensor', axis=1, tiled=True)]
    ppermute x0 -> x3, starting transfers between devices: none -> 32.7 us  [gather_around(): blocks.append(lax.ppermute(blocks[-1], axis, right))]
    psum x1, waiting for transfers between devices: 27.3 us -> 1.31 us  [body(): core_mat = lax.psum(core_part.astype(jnp.bfloat16), 'tensor')]
  transfers between devices with their start and end apart: 4 -> 6, of which waited for: 4 -> 6; matrix products, arithmetic and copies ran while one was open for 4% -> 6% of each run, Pallas kernels for 0% -> 0%
where the time goes in v1:
time: 522 us; the launch traced here: 521 us
  waiting for transfers between devices  175 us (34%)
  blocking collectives  119 us (23%)
  local copies, waits for them, and re-layouts  89.7 us (17%)
  other arithmetic  57.8 us (11%)
  starting transfers between devices  32.8 us (6%)
  matrix products  30.3 us (6%)
  between operations  16 us (3%)
    ppermute x3, waiting for transfers between devices, gather_around(): blocks.append(lax.ppermute(blocks[-1], axis, right))  96.5 us
    reduce_scatter x1, waiting for transfers between devices, body(): lax.psum_scatter(jnp.einsum('lrk,lrd->dlk', row_basis, group_block, prefe...  75.4 us
    all_to_all x1, blocking collectives, body(): lax.all_to_all(gradient, 'layer', split_axis=0, concat_axis=2, tiled=True)  54.5 us
    all_to_all x1, blocking collectives, body(): lax.all_to_all(rows_block, 'layer', split_axis=2, concat_axis=0, tiled=True)  53.6 us
    convert_element_type x1, local copies, waits for them, and re-layouts, finish(): return (raw_update * factor[:, None, None]).astype(jnp.bfloat16)  49.5 us
    unnamed x1, other arithmetic  43.5 us
    ppermute x3, starting transfers between devices, gather_around(): blocks.append(lax.ppermute(blocks[-1], axis, right))  32.7 us
    unnamed x16, local copies, waits for them, and re-layouts  22.3 us
  transfers between devices with their start and end apart: 6, of which 6 were waited for; matrix products, arithmetic and copies ran while one was open for 6% of the time, Pallas kernels for 0%

profile of v1, /device:TPU:0, one launch (start us, length us, event | category | flops | bytes accessed | tf_op | source)
XLA Modules:
  0.0 520.7 jit_solution(6145690399948642083)
XLA Ops:
  6.5 0.0 copy-start
  6.5 0.0 reduce-scatter.2.cloned.1.call-start
  6.5 54.5 %all_to_all.36 = bf16[8,256,1024]{2,1,0:T(8,128)(2,1)} all-to-all(bf16[8,256,1024]{2,1,0:T(8,128)(2,1)} %param.7), channel_id=1, replica_groups=mesh['layer'=8,'tensor'=4] {'layer'}, dimensions={0} | all-to-all | bytes 8388608 | tf_op jit(solution)/shard_map/all_to_all | solution.py:48
  61.0 6.4 %copy.15 = bf16[1,256,8,1024]{1,3,2,0:T(8,128)(2,1)} copy(bf16[1,256,8,1024]{3,1,2,0:T(8,128)(2,1)} %bitcast.88) | data formatting | bytes 8388608 | tf_op jit(solution)/shard_map/all_to_all | solution.py:48
  67.4 0.0 copy-done
  67.4 5.4 %fusion.2 = bf16[8192,1,256]{2,0,1:T(8,128)(2,1)} fusion(bf16[256,8192]{0,1:T(8,128)(2,1)} %bitcast.85, bf16[1,256,256]{2,1,0:T(8,128)(2,1)S(1)} %copy-done), kind=kOutput, calls=%fused_computation.6 | convolution fusion | flops 1075838976 | bytes 8519680 | tf_op jit(solution)/shard_map/lrk,lrd->dlk/dot_general | solution.py:51
  72.8 0.0 copy-start.4
  72.8 0.0 copy-start.5
  72.8 0.0 reduce-scatter.2.cloned.1.call-update
  72.9 0.0 all-gather.2.cloned.1.call-start
  72.9 0.7 all-gather.2.cloned.1.call-update
  73.6 0.0 all-reduce.3.cloned.1.call-start
  74.4 0.0 copy-done.4
  74.4 75.4 %reduce-scatter.2.cloned.1.call-done = bf16[2048,1,256]{2,0,1:T(8,128)(2,1)} async-done(((bf16[8192,1,256]{2,0,1:T(8,128)(2,1)}), bf16[2048,1,256]{2,0,1:T(8,128)(2,1)}) %reduce-scatter.2.cloned.1.call-update) | async-done | bytes 1048592 | tf_op jit(solution)/shard_map/reduce_scatter | solution.py:50
  149.8 1.4 multiply_convert_fusion.1
  151.3 1.6 collective-permute-start
  152.8 39.4 %collective-permute-done = bf16[2048,1,256]{2,0,1:T(8,128)(2,1)} collective-permute-done((bf16[2048,1,256]{2,0,1:T(8,128)(2,1)S(1)}, bf16[2048,1,256]{2,0,1:T(8,128)(2,1)}, u32[]{:S(2)}, u32[]{:S(2)}) %collective-permute-start) | collective-permute-done | bytes 1048608 | tf_op jit(solution)/shard_map/ppermute | solution.py:18
  192.3 18.1 %collective-permute-start.1 = (bf16[2048,1,256]{2,0,1:T(8,128)(2,1)}, bf16[2048,1,256]{2,0,1:T(8,128)(2,1)}, u32[]{:S(2)}, u32[]{:S(2)}) collective-permute-start(bf16[2048,1,256]{2,0,1:T(8,128)(2,1)} %collective-permute-done), channel_id=1, source_target_pairs={{0,1},{1,2},{2,3},{3,0},{4,5},{5,6},{6,7},{7,4},{8,9},{9,10},{10,1... | collective-permute-start | bytes 3145736 | tf_op jit(solution)/shard_map/ppermute | solution.py:18
  211.1 0.0 copy-done.5
  211.1 5.0 multiply_reduce_fusion.1
  216.1 0.0 copy-start.2
  216.1 0.0 copy-start.3
  216.1 38.0 %collective-permute-done.1 = bf16[2048,1,256]{2,0,1:T(8,128)(2,1)} collective-permute-done((bf16[2048,1,256]{2,0,1:T(8,128)(2,1)}, bf16[2048,1,256]{2,0,1:T(8,128)(2,1)}, u32[]{:S(2)}, u32[]{:S(2)}) %collective-permute-start.1) | collective-permute-done | bytes 1048608 | tf_op jit(solution)/shard_map/ppermute | solution.py:18
  254.1 13.1 %collective-permute-start.2 = (bf16[2048,1,256]{2,0,1:T(8,128)(2,1)}, bf16[2048,1,256]{2,0,1:T(8,128)(2,1)}, u32[]{:S(2)}, u32[]{:S(2)}) collective-permute-start(bf16[2048,1,256]{2,0,1:T(8,128)(2,1)} %collective-permute-done.1), channel_id=1, source_target_pairs={{0,1},{1,2},{2,3},{3,0},{4,5},{5,6},{6,7},{7,4},{8,9},{9,10},{10,1... | collective-permute-start | bytes 3145736 | tf_op jit(solution)/shard_map/ppermute | solution.py:18
  267.2 1.0 all-gather.2.cloned.1.call-done
  268.2 4.7 fusion.9
  272.9 0.0 copy-done.2
  272.9 1.1 convolution_convert_fusion.1
  274.1 0.0 all-reduce.3.cloned.1.call-update
  274.1 0.0 copy-done.3
  274.1 0.2 fusion.28
  274.3 19.0 %collective-permute-done.2 = bf16[2048,1,256]{2,0,1:T(8,128)(2,1)} collective-permute-done((bf16[2048,1,256]{2,0,1:T(8,128)(2,1)}, bf16[2048,1,256]{2,0,1:T(8,128)(2,1)}, u32[]{:S(2)}, u32[]{:S(2)}) %collective-permute-start.2) | collective-permute-done | bytes 1048608 | tf_op jit(solution)/shard_map/ppermute | solution.py:18
  293.3 3.6 maximum_bitcast_fusion
  296.9 5.0 gather_fusion
  301.9 8.0 %fusion.1 = f32[256,8192]{0,1:T(8,128)} fusion(bf16[8192,256]{1,0:T(8,128)(2,1)} %bitcast.91, bf16[256,8192]{0,1:T(8,128)(2,1)} %bitcast.87, f32[]{:T(128)} %bitcast.4, f32[]{:T(128)} %bitcast, bf16[1,256,256]{2,1,0:T(8,128)(2,1)S(1)} %copy-done), kind=kOutput, calls=%fused_computation.4 | convolution fusion | flops 1082130432 | bytes 16908296 | tf_op jit(solution)/shard_map/lrk,dlk->lrd/dot_general | solution.py:65
  309.9 1.3 all-reduce.3.cloned.1.call-done
  311.2 11.0 %multiply_reduce_fusion = (f32[]{:T(128)}, f32[256,8192]{0,1:T(8,128)}) fusion(f32[256,8192]{0,1:T(8,128)} %fusion.1, bf16[1,8192,256]{2,1,0:T(8,128)(2,1)} %all-gather.2.cloned.1.call-done, f32[256,256]{1,0:T(8,128)S(1)} %fusion.9, bf16[256,256]{1,0:T(8,128)(2,1)} %all-reduce.3.cloned.1.call-done, bf16[1,256,256]{2,1,0:T(8,128)(2,1)S(1)} %copy-done, ...), kind=kOutput, calls=%fused_computation.8 | convolution fusion | flops 1113784320 | bytes 21496836 | tf_op jit(solution)/shard_map/lrk,ldk->lrd/dot_general | solution.py:76
  322.2 11.3 %all-reduce = (f32[1]{0:T(128)}, f32[1]{0:T(128)}) all-reduce(f32[1]{0:T(128)} %bitcast.25, f32[1]{0:T(128)} %bitcast.26), channel_id=1, replica_groups=mesh['layer'=8,'tensor'=4] {'tensor'}, use_global_device_ids=true, to_apply=%region_3.0 | all-reduce | flops 2 | bytes 16 | tf_op jit(solution)/shard_map/psum | solution.py:34
  334.8 4.1 fusion.3
  338.8 49.5 %copy.24 = bf16[1,256,8192]{1,0,2:T(2,128)(2,1)} copy(bf16[1,256,8192]{1,2,0:T(8,128)(2,1)S(1)} %fusion.3) | data formatting | bytes 8388608 | tf_op jit(solution)/shard_map/convert_element_type | solution.py:40
  388.4 0.5 broadcast.92
  388.9 43.5 %reduce.4 = bf16[8192,256]{1,0:T(8,128)(2,1)} reduce(bf16[8192,1,256]{2,1,0:T(2,128)(2,1)} %bitcast.89, bf16[]{:T(256)} %broadcast.92), dimensions={1}, to_apply=%bitcast.82.reduce_sub_computation | reduce | bytes 8388610
  432.4 7.0 %reshape.152 = bf16[8,2,131072]{2,1,0:T(2,128)(2,1)} reshape(bf16[8192,256]{1,0:T(8,128)(2,1)} %reduce.4) | data formatting | bytes 8388608
  439.4 53.6 %all_to_all.37 = bf16[8,2,131072]{2,1,0:T(2,128)(2,1)} all-to-all(bf16[8,2,131072]{2,1,0:T(2,128)(2,1)} %reshape.152), channel_id=1, replica_groups=mesh['layer'=8,'tensor'=4] {'layer'}, dimensions={0} | all-to-all | bytes 8388608 | tf_op jit(solution)/shard_map/all_to_all | solution.py:80
  492.9 8.7 %reshape.153 = bf16[8192,1,256]{2,1,0:T(2,128)(2,1)} reshape(bf16[8,2,131072]{2,1,0:T(2,128)(2,1)} %all_to_all.37) | data formatting | bytes 8388608
  501.7 6.1 %copy.22 = bf16[1,256,8192]{1,2,0:T(8,128)(2,1)} copy(bf16[1,256,8192]{1,0,2:T(2,128)(2,1)} %bitcast.90) | data formatting | bytes 8388608
  507.7 6.5 %copy.19 = bf16[8,256,1024]{2,1,0:T(8,128)(2,1)} copy(bf16[8,256,1024]{1,2,0:T(8,128)(2,1)} %bitcast.92) | data formatting | bytes 8388608 | tf_op jit(solution)/shard_map/all_to_all | solution.py:80
  514.2 0.0 copy-done.1
  (5 shorter events, 0.0 us)
Async XLA Ops:
  6.5 60.9 %copy-start = (bf16[1,256,256]{2,1,0:T(8,128)(2,1)S(1)}, bf16[1,256,256]{2,1,0:T(8,128)(2,1)}, u32[]{:S(2)}) copy-start(bf16[1,256,256]{2,1,0:T(8,128)(2,1)} %param.8) | copy-start | bytes 393220
  6.5 143.3 %reduce-scatter.2.cloned.1.call-start = ((), (), s32[]{:S(2)}) async-start(), calls=%async_computation.3 | async-start | bytes 5242880 | tf_op jit(solution)/shard_map/reduce_scatter | solution.py:50
  72.8 1.5 copy-start.4
  72.8 138.2 %copy-start.5 = (f32[1,256]{1,0:T(1,128)S(1)}, f32[1,256]{1,0:T(1,128)}, u32[]{:S(2)}) copy-start(f32[1,256]{1,0:T(1,128)} %param.11) | copy-start | bytes 3076
  72.9 195.3 %all-gather.2.cloned.1.call-start = ((), (), s32[]{:S(2)}) async-start(), calls=%async_computation.4 | async-start | bytes 5242880 | tf_op jit(solution)/shard_map/all_gather | solution.py:61
  73.6 237.6 %all-reduce.3.cloned.1.call-start = ((), (), s32[]{:S(2)}) async-start(), calls=%async_computation.5 | async-start | bytes 262144 | tf_op jit(solution)/shard_map/psum | solution.py:60
  151.3 41.0 %collective-permute-start = (bf16[2048,1,256]{2,0,1:T(8,128)(2,1)S(1)}, bf16[2048,1,256]{2,0,1:T(8,128)(2,1)}, u32[]{:S(2)}, u32[]{:S(2)}) collective-permute-start(bf16[2048,1,256]{2,0,1:T(8,128)(2,1)S(1)} %multiply_convert_fusion.1), channel_id=1, source_target_pairs={{0,1},{1,2},{2,3},{3,0},{4,5},{5,6},{6,7},{7,4},{8,9},{9,10},{10,1... | collective-permute-start | bytes 3145736 | tf_op jit(solution)/shard_map/ppermute | solution.py:18
  192.3 61.8 %collective-permute-start.1 = (bf16[2048,1,256]{2,0,1:T(8,128)(2,1)}, bf16[2048,1,256]{2,0,1:T(8,128)(2,1)}, u32[]{:S(2)}, u32[]{:S(2)}) collective-permute-start(bf16[2048,1,256]{2,0,1:T(8,128)(2,1)} %collective-permute-done), channel_id=1, source_target_pairs={{0,1},{1,2},{2,3},{3,0},{4,5},{5,6},{6,7},{7,4},{8,9},{9,10},{10,1... | collective-permute-start | bytes 3145736 | tf_op jit(solution)/shard_map/ppermute | solution.py:18
  216.1 56.9 %copy-start.2 = (bf16[1,2048,256]{2,1,0:T(8,128)(2,1)S(1)}, bf16[1,2048,256]{2,1,0:T(8,128)(2,1)}, u32[]{:S(2)}) copy-start(bf16[1,2048,256]{2,1,0:T(8,128)(2,1)} %param.9) | copy-start | bytes 3145732
  216.1 58.0 %copy-start.3 = (bf16[2048,1,256]{2,0,1:T(8,128)(2,1)S(1)}, bf16[2048,1,256]{2,0,1:T(8,128)(2,1)}, u32[]{:S(2)}) copy-start(bf16[2048,1,256]{2,0,1:T(8,128)(2,1)} %reduce-scatter.2.cloned.1.call-done) | copy-start | bytes 3145732
  254.1 39.2 %collective-permute-start.2 = (bf16[2048,1,256]{2,0,1:T(8,128)(2,1)}, bf16[2048,1,256]{2,0,1:T(8,128)(2,1)}, u32[]{:S(2)}, u32[]{:S(2)}) collective-permute-start(bf16[2048,1,256]{2,0,1:T(8,128)(2,1)} %collective-permute-done.1), channel_id=1, source_target_pairs={{0,1},{1,2},{2,3},{3,0},{4,5},{5,6},{6,7},{7,4},{8,9},{9,10},{10,1... | collective-permute-start | bytes 3145736 | tf_op jit(solution)/shard_map/ppermute | solution.py:18
  507.7 6.5 %copy-start.1 = (bf16[1,256,256]{2,1,0:T(8,128)(2,1)S(1)}, bf16[1,256,256]{2,1,0:T(8,128)(2,1)}, u32[]{:S(2)}) copy-start(bf16[1,256,256]{2,1,0:T(8,128)(2,1)} %param.8) | copy-start | bytes 393220
Sparse Core Ops, SparseCore 0:
  73.0 76.7 reduce-scatter.1
  151.4 116.7 all-gather.1
  274.2 36.9 all-reduce.2
